TPU v7x, 256 devices: a whole 4x4x8 slice. The times are simulated.
256 devices in a mesh: replica: 8 (over y, x_hi), fsdp: 32 (over z, x_lo, core).
Axes of the slice: x: 4 (x_hi: 2, x_lo: 2; x = x_hi * 2 + x_lo), y: 4, z: 8, core: 2. Of those that a mesh axis runs over, the one named last changes fastest.
Arguments:
- partner: int32 [8], replicated, may hold values from 0 to 7, as said below
- tokens: bfloat16 [8, 512, 4096], P('replica', 'fsdp'), may hold values from -6 to 6
- w_gate: bfloat16 [8, 7168, 4096], P('replica', 'fsdp'), may hold values from -0.09375 to 0.09375
- w_up: bfloat16 [8, 7168, 4096], P('replica', 'fsdp'), may hold values from -0.09375 to 0.09375
- w_down: bfloat16 [8, 7168, 4096], P('replica', 'fsdp'), may hold values from -0.0625 to 0.0625
Outputs:
- grad_gate: bfloat16 [8, 7168, 4096], P('replica', 'fsdp')
- grad_up: bfloat16 [8, 7168, 4096], P('replica', 'fsdp')
- grad_down: bfloat16 [8, 7168, 4096], P('replica', 'fsdp')
Inputs may be any that keep to these rules, and one draw needn't show every extreme that they name: partner is a permutation of the 8 replicas that forms one single cycle through all of them; no replica is its own partner.
All inputs are finite; a program needn't handle non-finite values.
Results may differ from a plain program's by a relative error of at most 0.025.
Values may be sent and summed in bfloat16 or wider, within the bound.
A program may use at most 128 MiB of HBM per device.

v0:
```python
import math

import jax
import jax.numpy as jnp
from jax import lax
from jax.sharding import Mesh
from jax.sharding import PartitionSpec as P

REPLICA = ("replica_0", "replica_1")


def cut_along(value, dim, devices):
    dims = value.shape
    parts = value.reshape(*dims[:dim], devices, dims[dim] // devices, *dims[dim + 1 :])
    return jnp.moveaxis(parts, dim, 0)


def in_order(parts, dim):
    dims = list(parts.shape[1:])
    dims[dim] *= parts.shape[0]
    return jnp.moveaxis(parts, 0, dim).reshape(dims)


def moved_by_axis(parts, axes, order):
    inside = parts.shape[1:]
    filled = parts.reshape(*(lax.axis_size(a) for a in axes), *inside)
    for k in order:
        filled = lax.all_to_all(filled, axes[k], k, k, tiled=True)
    return filled.reshape(-1, *inside)


def one_axis_at_a_time(value, axes, order, split_dim, concat_dim):
    parts = cut_along(value, split_dim, lax.axis_size(axes))
    return in_order(moved_by_axis(parts, axes, order), concat_dim)


def in_one_piece(arrays, axis, dim, along):
    widths = [a.shape[along] for a in arrays]
    both = jnp.concatenate(arrays, axis=along)
    filled = lax.all_gather(both, axis, axis=dim, tiled=True)
    return tuple(jnp.split(filled, [sum(widths[:k]) for k in range(1, len(widths))], axis=along))


def side_by_side(arrays, axis, dim, along):
    widths = [a.shape[along] for a in arrays]
    both = jnp.concatenate(arrays, axis=along)
    filled = lax.psum_scatter(both, axis, scatter_dimension=dim, tiled=True)
    return tuple(jnp.split(filled, [sum(widths[:k]) for k in range(1, len(widths))], axis=along))


def contract(left, right, left_dim, right_dim):
    return lax.dot_general(
        left, right, (((left_dim,), (right_dim,)), ((), ())), preferred_element_type=jnp.float32
    )


def forward_pass(rows_all, gate_w, up_w, down_w):
    pre_gate = contract(gate_w, rows_all, 1, 1)
    pre_up = contract(up_w, rows_all, 1, 1)
    hidden = (jax.nn.silu(pre_gate) * pre_up).astype(jnp.bfloat16)
    partial_value = contract(hidden, down_w, 0, 0)
    return (pre_gate, pre_up, hidden, partial_value)


def local(partner, tokens, w_gate, w_up, w_down):
    own_rows = tokens[0]
    replicas = lax.axis_size(REPLICA)
    members = lax.axis_size("fsdp")
    loss_scale = 1.0 / math.sqrt(own_rows.shape[0] * members)
    indices = jnp.arange(replicas, dtype=jnp.int32)
    matches = (partner[:, None] == indices[None, :]).astype(jnp.int32)
    inverse = jnp.sum(indices[:, None] * matches, axis=0)
    row_spread = one_axis_at_a_time(own_rows[None], REPLICA, (0, 1), 2, 0)
    row_chosen = jnp.take(row_spread, inverse, axis=0)
    foreign_rows = lax.all_to_all(row_chosen, REPLICA, split_axis=0, concat_axis=2, tiled=True)
    rows_all, foreign_all = in_one_piece((own_rows, foreign_rows[0]), "fsdp", 0, 1)
    pre_gate, pre_up, hidden, student_part = forward_pass(rows_all, w_gate[0], w_up[0], w_down[0])
    teacher_part = forward_pass(foreign_all, w_gate[0], w_up[0], w_down[0])[3]
    student, teacher_sum = tuple(
        (
            part.astype(jnp.float32)
            for part in side_by_side(
                (student_part.astype(jnp.bfloat16), teacher_part.astype(jnp.bfloat16)), "fsdp", 0, 1
            )
        )
    )
    result_spread = lax.all_to_all(
        teacher_sum[None].astype(jnp.bfloat16), REPLICA, split_axis=2, concat_axis=0, tiled=True
    ).astype(jnp.float32)
    result_chosen = jnp.take(result_spread, partner, axis=0)
    teacher = lax.all_to_all(
        result_chosen.astype(jnp.bfloat16), REPLICA, split_axis=0, concat_axis=2, tiled=True
    ).astype(result_chosen.dtype)[0]
    cotangent = ((student - teacher) * loss_scale).astype(jnp.bfloat16)
    cotangent_all = lax.all_gather(cotangent, "fsdp", axis=0, tiled=True)
    grad_down = contract(hidden, cotangent_all, 1, 0).astype(jnp.bfloat16)
    d_hidden = contract(w_down[0], cotangent_all, 1, 1)
    sigma = jax.nn.sigmoid(pre_gate)
    d_gate = (d_hidden * pre_up * sigma * (1.0 + pre_gate * (1.0 - sigma))).astype(jnp.bfloat16)
    d_up = (d_hidden * pre_gate * sigma).astype(jnp.bfloat16)
    grad_gate = contract(d_gate, rows_all, 1, 0).astype(jnp.bfloat16)
    grad_up = contract(d_up, rows_all, 1, 0).astype(jnp.bfloat16)
    return (grad_gate[None], grad_up[None], grad_down[None])


def solution(mesh):
    split = Mesh(mesh.devices.reshape(4, 2, mesh.shape["fsdp"]), ("replica_0", "replica_1", "fsdp"))
    in_specs = (
        P(),
        P(REPLICA, "fsdp", None),
        P(REPLICA, "fsdp", None),
        P(REPLICA, "fsdp", None),
        P(REPLICA, "fsdp", None),
    )
    out_specs = (P(REPLICA, "fsdp", None), P(REPLICA, "fsdp", None), P(REPLICA, "fsdp", None))
    return jax.shard_map(local, mesh=split, in_specs=in_specs, out_specs=out_specs, check_vma=False)
```

profile of v0, /device:TPU:1, one launch (start us, length us, event | category | flops | bytes accessed | tf_op | source)
XLA Modules:
  0.0 421.7 jit_solution(6102265696110842292)
XLA Ops:
  7.2 0.0 copy-start
  7.2 1.7 copy.54
  8.9 5.0 %all-to-all-start = ((bf16[4,2,1,16,512]{4,3,1,2,0:T(8,128)(2,1)}), bf16[4,2,1,16,512]{4,3,1,2,0:T(8,128)(2,1)S(1)}, u32[]{:S(2)}, u32[]{:S(2)}) async-start(bf16[4,2,1,16,512]{4,3,1,2,0:T(8,128)(2,1)} %bitcast.2), calls=%async_computation | async-start | bytes 262144 | tf_op jit(solution)/shard_map/all_to_all | solution.py:28
  13.9 0.7 select_reduce_fusion
  14.6 4.1 all-to-all-done
  18.7 0.7 copy.38
  19.4 4.0 all-to-all-start.1
  23.4 0.0 all-gather.3.cloned.1.call-start
  23.4 4.8 %all-to-all-done.1 = bf16[4,2,1,16,512]{4,3,0,2,1:T(8,128)(2,1)S(1)} async-done(((bf16[4,2,1,16,512]{4,3,0,2,1:T(8,128)(2,1)}), bf16[4,2,1,16,512]{4,3,0,2,1:T(8,128)(2,1)S(1)}, u32[]{:S(2)}, u32[]{:S(2)}) %all-to-all-start.1) | async-done | bytes 131104 | tf_op jit(solution)/shard_map/all_to_all | solution.py:28
  28.2 0.6 gather_fusion
  28.8 0.1 broadcast_select_fusion
  28.9 9.4 %all_to_all.43 = bf16[8,16,512]{2,1,0:T(8,128)(2,1)S(1)} all-to-all(bf16[8,16,512]{2,1,0:T(8,128)(2,1)S(1)} %broadcast_select_fusion), channel_id=1, replica_groups=mesh['replica_0'=4,'replica_1'=2,'fsdp'=32] {'replica_0','replica_1'}, dimensions={0} | all-to-all | bytes 262144 | tf_op jit(solution)/shard_map/all_to_all | solution.py:75
  38.3 1.6 pad_maximum_fusion.1
  40.0 0.0 all-gather.3.cloned.1.call-update
  40.0 0.0 reduce-scatter.2.cloned.1.call-start
  40.0 74.8 %all-gather.3.cloned.1.call-done = bf16[512,8192]{1,0:T(8,128)(2,1)} async-done(((bf16[16,8192]{1,0:T(8,128)(2,1)}), bf16[512,8192]{1,0:T(8,128)(2,1)}) %all-gather.3.cloned.1.call-update) | async-done | bytes 8388624 | tf_op jit(solution)/shard_map/all_gather | solution.py:40
  114.9 0.0 copy-start.3
  114.9 4.3 %fusion.24 = f32[224,512]{1,0:T(8,128)S(1)} fusion(bf16[1,224,4096]{2,1,0:T(8,128)(2,1)} %param.7, bf16[512,8192]{1,0:T(8,128)(2,1)} %all-gather.3.cloned.1.call-done), kind=kOutput, calls=%fused_computation.30 | convolution fusion | flops 939524096 | bytes 6488064 | tf_op jit(solution)/shard_map/dot_general | solution.py:52
  119.2 0.8 copy-done.3
  120.1 0.0 copy-start.6
  120.1 3.9 multiply_convert_fusion.2
  123.9 0.0 copy-done.6
  123.9 0.0 copy-start.4
  123.9 0.0 copy-done
  123.9 3.3 convolution_convert_fusion.1
  127.2 0.0 copy-done.4
  127.2 1.4 fusion.34
  128.6 7.4 %convolution_convert_fusion = bf16[512,4096]{1,0:T(8,128)(2,1)} fusion(bf16[1,224,4096]{2,1,0:T(8,128)(2,1)S(1)} %copy-done, bf16[1,224,4096]{2,1,0:T(8,128)(2,1)} %param.8, bf16[512,8192]{1,0:T(8,128)(2,1)} %all-gather.3.cloned.1.call-done, f32[224,512]{1,0:T(8,128)S(1)} %fusion.34), kind=kOutput, calls=%fused_computation.3 | convolution fusion | flops 1881833472 | bytes 12517376 | tf_op jit(solution)/shard_map/dot_general | solution.py:52
  136.1 7.7 %pad_maximum_fusion = bf16[512,8192]{1,0:T(8,128)(2,1)} fusion(bf16[512,4096]{1,0:T(8,128)(2,1)} %convolution_convert_fusion, bf16[512,4096]{1,0:T(8,128)(2,1)} %convolution_convert_fusion.1), kind=kLoop, calls=%fused_computation.2 | loop fusion | flops 16777216 | bytes 16777216 | tf_op jit(solution)/shard_map/concatenate | solution.py:46
  143.8 0.0 copy-start.5
  143.8 0.0 reduce-scatter.2.cloned.1.call-update
  143.8 0.6 copy-done.5
  144.4 126.9 %reduce-scatter.2.cloned.1.call-done = bf16[16,8192]{1,0:T(8,128)(2,1)} async-done(((bf16[512,8192]{1,0:T(8,128)(2,1)}), bf16[16,8192]{1,0:T(8,128)(2,1)}) %reduce-scatter.2.cloned.1.call-update) | async-done | bytes 262160 | tf_op jit(solution)/shard_map/reduce_scatter | solution.py:47
  271.4 0.9 slice_bitcast_fusion
  272.3 4.0 copy.41
  276.3 0.5 broadcast.61
  276.8 23.4 %reduce = bf16[4096,16]{1,0:T(8,128)(2,1)S(1)} reduce(bf16[4096,1,16]{2,1,0:T(2,128)(2,1)} %bitcast.109, bf16[]{:T(256)} %broadcast.61), dimensions={1}, to_apply=%bitcast.93.reduce_sub_computation | reduce | bytes 262146
  300.2 0.0 copy-start.2
  300.2 1.7 reshape.69
  302.0 6.0 %all-to-all-start.3 = ((bf16[8,2,4096]{2,1,0:T(2,128)(2,1)}), bf16[8,2,4096]{2,1,0:T(2,128)(2,1)S(1)}, u32[]{:S(2)}, u32[]{:S(2)}) async-start(bf16[8,2,4096]{2,1,0:T(2,128)(2,1)} %reshape.69), calls=%async_computation.4 | async-start | bytes 262144 | tf_op jit(solution)/shard_map/all_to_all | solution.py:87
  308.0 0.0 all-gather.5.cloned.1.call-start
  308.1 7.0 %all-to-all-done.3 = bf16[8,2,4096]{2,1,0:T(2,128)(2,1)S(1)} async-done(((bf16[8,2,4096]{2,1,0:T(2,128)(2,1)}), bf16[8,2,4096]{2,1,0:T(2,128)(2,1)S(1)}, u32[]{:S(2)}, u32[]{:S(2)}) %all-to-all-start.3) | async-done | bytes 131104 | tf_op jit(solution)/shard_map/all_to_all | solution.py:87
  315.0 3.9 reshape.70
  319.0 4.4 %copy.42 = bf16[1,16,4096]{2,1,0:T(8,128)(2,1)S(1)} copy(bf16[1,16,4096]{1,0,2:T(2,128)(2,1)} %bitcast.110) | data formatting | bytes 262144 | tf_op jit(solution)/shard_map/all_to_all | solution.py:87
  323.4 0.6 gather_fusion.1
  324.0 0.1 select_convert_fusion
  324.1 9.4 %all_to_all.44 = bf16[8,16,512]{2,1,0:T(8,128)(2,1)S(1)} all-to-all(bf16[8,16,512]{2,1,0:T(8,128)(2,1)S(1)} %select_convert_fusion), channel_id=1, replica_groups=mesh['replica_0'=4,'replica_1'=2,'fsdp'=32] {'replica_0','replica_1'}, dimensions={0} | all-to-all | bytes 262144 | tf_op jit(solution)/shard_map/all_to_all | solution.py:91
  333.6 0.0 copy-done.2
  333.6 0.7 multiply_convert_fusion.3
  334.3 0.0 all-gather.5.cloned.1.call-update
  334.3 67.5 %all-gather.5.cloned.1.call-done = bf16[512,4096]{1,0:T(8,128)(2,1)} async-done(((bf16[16,4096]{1,0:T(8,128)(2,1)}), bf16[512,4096]{1,0:T(8,128)(2,1)}) %all-gather.5.cloned.1.call-update) | async-done | bytes 4194320 | tf_op jit(solution)/shard_map/all_gather | solution.py:95
  401.8 0.0 copy-start.1
  401.8 4.7 %fusion.2 = bf16[1,224,4096]{2,1,0:T(8,128)(2,1)} fusion(bf16[224,512]{1,0:T(8,128)(2,1)S(1)} %get-tuple-element.3, bf16[512,4096]{1,0:T(8,128)(2,1)} %all-gather.5.cloned.1.call-done), kind=kOutput, calls=%fused_computation.10 | convolution fusion | flops 940441600 | bytes 6258688 | tf_op jit(solution)/shard_map/dot_general | solution.py:52
  406.5 0.0 copy-done.1
  406.5 0.0 copy-start.7
  406.5 1.4 fusion.21
  408.0 0.0 copy-done.7
  408.0 0.0 slice-start.1
  408.0 0.0 copy-start.8
  408.0 4.7 %fusion.1 = bf16[1,224,4096]{2,1,0:T(8,128)(2,1)} fusion(bf16[512,8192]{1,0:T(8,128)(2,1)} %all-gather.3.cloned.1.call-done, f32[224,512]{1,0:T(8,128)S(1)} %fusion.21, f32[224,512]{1,0:T(8,128)S(1)} %copy-done.7), kind=kOutput, calls=%fused_computation.9 | convolution fusion | flops 941129728 | bytes 6946816 | tf_op jit(solution)/shard_map/dot_general | solution.py:52
  412.7 0.0 slice-done
  412.8 0.0 slice-done.1
  412.8 0.0 copy-done.8
  412.8 2.4 fusion
  (13 shorter events, 0.1 us)
Async XLA Ops:
  7.2 116.8 %copy-start = (bf16[1,224,4096]{2,1,0:T(8,128)(2,1)S(1)}, bf16[1,224,4096]{2,1,0:T(8,128)(2,1)}, u32[]{:S(2)}) copy-start(bf16[1,224,4096]{2,1,0:T(8,128)(2,1)} %param.9) | copy-start | bytes 5505028
  8.9 9.8 %all-to-all-start = ((bf16[4,2,1,16,512]{4,3,1,2,0:T(8,128)(2,1)}), bf16[4,2,1,16,512]{4,3,1,2,0:T(8,128)(2,1)S(1)}, u32[]{:S(2)}, u32[]{:S(2)}) async-start(bf16[4,2,1,16,512]{4,3,1,2,0:T(8,128)(2,1)} %bitcast.2), calls=%async_computation | async-start | bytes 262144 | tf_op jit(solution)/shard_map/all_to_all | solution.py:28
  19.4 8.8 %all-to-all-start.1 = ((bf16[4,2,1,16,512]{4,3,0,2,1:T(8,128)(2,1)}), bf16[4,2,1,16,512]{4,3,0,2,1:T(8,128)(2,1)S(1)}, u32[]{:S(2)}, u32[]{:S(2)}) async-start(bf16[4,2,1,16,512]{4,3,0,2,1:T(8,128)(2,1)} %copy.38), calls=%async_computation.1 | async-start | bytes 262144 | tf_op jit(solution)/shard_map/all_to_all | solution.py:28
  23.4 91.5 %all-gather.3.cloned.1.call-start = ((), (), s32[]{:S(2)}) async-start(), calls=%async_computation.6 | async-start | bytes 8650752 | tf_op jit(solution)/shard_map/all_gather | solution.py:40
  40.0 231.4 %reduce-scatter.2.cloned.1.call-start = ((), (), s32[]{:S(2)}) async-start(), calls=%async_computation.7 | async-start | bytes 8650752 | tf_op jit(solution)/shard_map/reduce_scatter | solution.py:47
  114.9 5.2 %copy-start.3 = (bf16[512,8192]{1,0:T(8,128)(2,1)S(1)}, bf16[512,8192]{1,0:T(8,128)(2,1)}, u32[]{:S(2)}) copy-start(bf16[512,8192]{1,0:T(8,128)(2,1)} %all-gather.3.cloned.1.call-done) | copy-start | bytes 25165828
  120.1 3.9 copy-start.6
  123.9 3.3 copy-start.4
  143.8 0.7 copy-start.5
  300.2 33.3 %copy-start.2 = (bf16[16,8192]{1,0:T(8,128)(2,1)S(1)}, bf16[16,8192]{1,0:T(8,128)(2,1)}, u32[]{:S(2)}) copy-start(bf16[16,8192]{1,0:T(8,128)(2,1)} %reduce-scatter.2.cloned.1.call-done) | copy-start | bytes 786436
  302.0 13.1 %all-to-all-start.3 = ((bf16[8,2,4096]{2,1,0:T(2,128)(2,1)}), bf16[8,2,4096]{2,1,0:T(2,128)(2,1)S(1)}, u32[]{:S(2)}, u32[]{:S(2)}) async-start(bf16[8,2,4096]{2,1,0:T(2,128)(2,1)} %reshape.69), calls=%async_computation.4 | async-start | bytes 262144 | tf_op jit(solution)/shard_map/all_to_all | solution.py:87
  308.0 93.8 %all-gather.5.cloned.1.call-start = ((), (), s32[]{:S(2)}) async-start(), calls=%async_computation.8 | async-start | bytes 4325376 | tf_op jit(solution)/shard_map/all_gather | solution.py:95
  401.8 4.7 %copy-start.1 = (bf16[512,4096]{1,0:T(8,128)(2,1)S(1)}, bf16[512,4096]{1,0:T(8,128)(2,1)}, u32[]{:S(2)}) copy-start(bf16[512,4096]{1,0:T(8,128)(2,1)} %all-gather.5.cloned.1.call-done) | copy-start | bytes 12582916
  406.5 1.4 copy-start.7
  406.5 6.2 %slice-start = ((s8[8388608]{0:T(1024)(128)(4,1)}), s8[4194304]{0:T(1024)(128)(4,1)S(1)}, s32[]{:S(2)}) async-start(s8[8388608]{0:T(1024)(128)(4,1)} %bitcast.119), calls=%async_computation.9 | async-start | bytes 8388608
  408.0 4.8 %slice-start.1 = ((s8[8388608]{0:T(1024)(128)(4,1)}), s8[4194304]{0:T(1024)(128)(4,1)S(1)}, s32[]{:S(2)}) async-start(s8[8388608]{0:T(1024)(128)(4,1)} %bitcast.119), calls=%async_computation.10 | async-start | bytes 8388608
  408.0 4.8 %copy-start.8 = (f32[224,512]{1,0:T(8,128)S(1)}, f32[224,512]{1,0:T(8,128)}, u32[]{:S(2)}) copy-start(f32[224,512]{1,0:T(8,128)} %get-tuple-element.4) | copy-start | bytes 1376260
Sparse Core Ops, SparseCore 0:
  40.1 74.7 all-gather.2
  143.9 127.4 reduce-scatter.1
  334.4 67.3 all-gather.4
where the time goes:
time: 422 us
  waiting for transfers between devices  285 us (68%)
  other arithmetic  34.4 us (8%)
  matrix products  33.6 us (8%)
  local copies, waits for them, and re-layouts  20.5 us (5%)
  blocking collectives  18.9 us (4%)
  starting transfers between devices  15.1 us (4%)
  between operations  13.9 us (3%)
    reduce_scatter x1, waiting for transfers between devices, side_by_side(): filled = lax.psum_scatter(both, axis, scatter_dimension=dim, tiled=True)  127 us
    all_gather x1, waiting for transfers between devices, in_one_piece(): filled = lax.all_gather(both, axis, axis=dim, tiled=True)  74.8 us
    all_gather x1, waiting for transfers between devices, local(): cotangent_all = lax.all_gather(cotangent, 'fsdp', axis=0, tiled=True)  67.5 us
    dot_general x9, matrix products, contract(): lax.dot_general(left, right, (((left_dim,), (right_dim,)), ((), ())), pre...  33.6 us
    unnamed x3, other arithmetic  23.5 us
    all_to_all x1, blocking collectives, local(): lax.all_to_all(row_chosen, REPLICA, split_axis=0, concat_axis=2, tiled=True)  9.44 us
    all_to_all x1, blocking collectives, local(): lax.all_to_all(result_chosen.astype(jnp.bfloat16), REPLICA, split_axis=0,...  9.44 us
    all_to_all x2, starting transfers between devices, moved_by_axis(): filled = lax.all_to_all(filled, axes[k], k, k, tiled=True)  9.01 us
  transfers between devices with their start and end apart: 6, of which 6 were waited for; matrix products, arithmetic and copies ran while one was open for 0% of the time, Pallas kernels for 0%

commit v1 on v0

v1 whole, which is shorter than its diff:
```python
import functools
import math

import jax
import jax.numpy as jnp
from jax import lax
from jax.experimental import pallas as pl
from jax.experimental.pallas import tpu as pltpu
from jax.sharding import Mesh
from jax.sharding import PartitionSpec as P

MESH = pl.DeviceIdType.MESH
REPLICA = ("ry", "rx")
FSDP = ("z", "x", "c")
BF = jnp.bfloat16
F32 = jnp.float32


class Place:
    def __init__(self, sizes):
        self.ry, self.rx, self.z, self.x, self.c = (lax.axis_index(a) for a in REPLICA + FSDP)
        self.deep, self.wide, self.copies = sizes["z"], sizes["rx"], sizes["ry"] * sizes["rx"]
        self.half = self.deep // 2
        self.replica = self.ry * self.wide + self.rx
        self.xn = {"x": 1 - self.x}
        self.cn = {"c": 1 - self.c}
        self.zn = {"+": {"z": self.at(1)}, "-": {"z": self.at(-1)}}

    def at(self, offset):
        return lax.rem(self.z + offset + self.deep, self.deep)

    def block(self, z, x, c):
        return (z * 2 + x) * 2 + c

    def other(self, offset):
        return lax.rem(self.replica + offset, self.copies)

    def peer(self, replica):
        return {"ry": replica // self.wide, "rx": lax.rem(replica, self.wide)}


class Wires:
    def __init__(self, send_sems, recv_sems, anyone):
        self.send_sems, self.recv_sems, self.anyone = send_sems, recv_sems, anyone
        self.keys, self.started = {}, []

    def key(self, key):
        return self.recv_sems.at[self.keys.setdefault(key, len(self.keys))]

    def send(self, src, dst, to, key):
        copy = pltpu.make_async_remote_copy(
            src_ref=src,
            dst_ref=dst,
            send_sem=self.send_sems.at[len(self.started)],
            recv_sem=self.key(key),
            device_id=to,
            device_id_type=MESH,
        )
        copy.start()
        self.started.append(copy)

    def wait(self, ref, key):
        pltpu.make_async_remote_copy(
            src_ref=ref,
            dst_ref=ref,
            send_sem=self.send_sems.at[0],
            recv_sem=self.key(key),
            device_id=self.anyone,
            device_id_type=MESH,
        ).wait_recv()

    def drain(self):
        for copy in self.started:
            copy.wait_send()


def greet(p):
    barrier = pltpu.get_barrier_semaphore()
    friends = [p.xn, p.cn, p.zn["+"], p.zn["-"]]
    friends += [p.peer(p.other(o)) for o in range(1, p.copies)]
    for friend in friends:
        pl.semaphore_signal(barrier, inc=1, device_id=friend, device_id_type=MESH)
    pl.semaphore_wait(barrier, len(friends))


def hops_of(half):
    reach = {}
    for name in ("a1", "o"):
        reach["+", name], reach["-", name] = half, half - 1
    for name in ("a2", "t"):
        reach["+", name], reach["-", name] = half - 1, half
    return reach


NAMES = ("a1", "a2", "o", "t")


def gather(w, tag, full, p):
    q = full.shape[-1] // 4
    cols = {"a1": pl.ds(0, q), "a2": pl.ds(q, q), "o": pl.ds(2 * q, 2 * q), "t": pl.ds(2 * q, 2 * q)}
    reach = hops_of(p.half)
    whole = pl.ds(0, 4 * q)
    steps, arrivals = [], []

    def piece(z, x, c, name):
        return full.at[p.block(z, x, c), :, whole if name == "all" else cols[name]]

    def put(z, x, name, to, key):
        ref = piece(z, x, p.c, name)
        w.send(ref, ref, to, key)

    def share(z, x, name, key):
        put(z, x, name, p.cn, (tag, "c") + key)
        arrivals.append((z, x, name, (tag, "c") + key))

    def own():
        put(p.z, p.x, "o", p.xn, (tag, "xb"))
        for name in ("a1", "a2", "o"):
            for way in "+-":
                put(p.z, p.x, name, p.zn[way], (tag, way, 1, name))
        for name in ("a1", "a2"):
            put(p.z, p.x, name, p.xn, (tag, "xa", "+", 0, name))
        share(p.z, p.x, "all", ("own",))

    def crossed():
        w.wait(piece(p.z, 1 - p.x, p.c, "t"), (tag, "xb"))
        for way in "+-":
            put(p.z, 1 - p.x, "t", p.zn[way], (tag, way, 1, "t"))
        share(p.z, 1 - p.x, "t", ("xb",))

    def from_x(way, s, name):
        z = p.at(-s if way == "+" else s)
        w.wait(piece(z, 1 - p.x, p.c, name), (tag, "xa", way, s, name))
        share(z, 1 - p.x, name, ("xa", way, s, name))

    def from_z(way, s, name):
        z = p.at(-s if way == "+" else s)
        x = 1 - p.x if name == "t" else p.x
        w.wait(piece(z, x, p.c, name), (tag, way, s, name))
        if s < reach[way, name]:
            put(z, x, name, p.zn[way], (tag, way, s + 1, name))
        if name in ("a1", "a2"):
            put(z, x, name, p.xn, (tag, "xa", way, s, name))
        share(z, x, name, (way, s, name))

    def last():
        for z, x, name, key in list(arrivals):
            w.wait(piece(z, x, 1 - p.c, name), key)

    steps += [own, crossed]
    steps += [functools.partial(from_x, "+", 0, name) for name in ("a1", "a2")]
    for s in range(1, p.half + 1):
        for name in NAMES:
            for way in "+-":
                if s <= reach[way, name]:
                    steps.append(functools.partial(from_z, way, s, name))
        for name in ("a1", "a2"):
            for way in "+-":
                if 1 <= s - 1 <= reach[way, name]:
                    steps.append(functools.partial(from_x, way, s - 1, name))
    for name in ("a1", "a2"):
        for way in "+-":
            if p.half <= reach[way, name]:
                steps.append(functools.partial(from_x, way, p.half, name))
    steps.append(last)
    return steps


def exchange(w, tag, src, spread, chosen, dst, pick, p):
    width = src.shape[-1] // p.copies

    def chunk(k):
        return pl.ds(pl.multiple_of(k * width, width), width)

    def out():
        for o in range(1, p.copies):
            k = p.other(o)
            w.send(src.at[:, chunk(k)], spread.at[p.replica], p.peer(k), (tag, "out", o))
        spread[p.replica] = src[:, chunk(p.replica)]

    def through():
        for o in range(1, p.copies):
            w.wait(spread.at[p.other(p.copies - o)], (tag, "out", o))
        for o in range(1, p.copies):
            r = p.other(o)
            chosen[o] = spread[pick(r)]
            w.send(chosen.at[o], dst.at[:, chunk(p.replica)], p.peer(r), (tag, "back", o))
        dst[:, chunk(p.replica)] = spread[pick(p.replica)]

    def back():
        for o in range(1, p.copies):
            w.wait(dst.at[:, chunk(p.other(p.copies - o))], (tag, "back", o))

    return [out, through, back]


def scatter(w, tag, part, got_c, put_x, got_x, put_z, got_z, put_b, got_b, p, finish):
    q = part.shape[-1] // 4
    a = pl.ds(0, 2 * q)
    cols = {"a1": pl.ds(0, q), "a2": pl.ds(q, q), "o": pl.ds(2 * q, 2 * q), "t": pl.ds(2 * q, 2 * q)}
    slot = {"a1": pl.ds(0, q), "a2": pl.ds(q, q), "o": pl.ds(2 * q, 2 * q), "t": pl.ds(4 * q, 2 * q)}
    reach = hops_of(p.half)
    index = {"+": 0, "-": 1}
    steps = []
    seen = set()

    def pair(z, x, where):
        return part[z, x, p.c, :, where].astype(F32) + got_c[z, x, :, where].astype(F32)

    def offsets(d):
        return (0,) if d == 0 else ((d,) if d == p.half else (d, -d))

    def halves():
        for d in range(p.half, -1, -1):
            for o in offsets(d):
                z = p.at(o)
                w.send(part.at[z, :, 1 - p.c], got_c.at[z], p.cn, (tag, "c", o))

    def cross(o):
        z = p.at(o)
        w.wait(got_c.at[z], (tag, "c", o))
        put_x[z] = pair(z, 1 - p.x, a).astype(BF)
        w.send(put_x.at[z], got_x.at[z], p.xn, (tag, "x", o))

    def value(z, name, where):
        x = 1 - p.x if name == "t" else p.x
        total = pair(z, x, where)
        if name in ("a1", "a2"):
            total += got_x[z, :, where].astype(F32)
        return total

    def arrived(o, name):
        if name in ("a1", "a2") and o not in seen:
            seen.add(o)
            w.wait(got_x.at[p.at(o)], (tag, "x", o))

    def came(way, d, name):
        ref = got_z.at[index[way], d - 1, :, slot[name]]
        w.wait(ref, (tag, way, d, name))
        return ref[...].astype(F32)

    def onward(way, d, name):
        o = d if way == "+" else (p.half if d == p.half else -d)
        z = p.at(o)
        arrived(o, name)
        total = value(z, name, cols[name])
        if d < reach[way, name]:
            total += came(way, d + 1, name)
        ref = put_z.at[index[way], d - 1, :, slot[name]]
        ref[...] = total.astype(BF)
        w.send(ref, got_z.at[index[way], d - 1, :, slot[name]], p.zn[way], (tag, way, d, name))

    def ended(name):
        arrived(0, name)
        total = value(p.z, name, cols[name])
        for way in "+-":
            if 1 <= reach[way, name]:
                total += came(way, 1, name)
        return total

    def hand():
        put_b[...] = ended("t").astype(BF)
        w.send(put_b, got_b, p.xn, (tag, "b"))
        finish(cols["a1"], ended("a1"))
        finish(cols["a2"], ended("a2"))

    def last():
        total = ended("o")
        w.wait(got_b, (tag, "b"))
        finish(cols["o"], total + got_b[...].astype(F32))

    steps.append(halves)
    for d in range(p.half, 0, -1):
        steps += [functools.partial(cross, o) for o in offsets(d)]
        for name in ("t", "o", "a1", "a2"):
            for way in "+-":
                if d <= reach[way, name]:
                    steps.append(functools.partial(onward, way, d, name))
    steps += [functools.partial(cross, 0), hand, last]
    return steps


def token_kernel(sizes, partner, tokens, full, spread, chosen, load_sem, send_sems, recv_sems):
    p = Place(sizes)
    me = p.block(p.z, p.x, p.c)
    load = pltpu.make_async_copy(tokens, full.at[0, me], load_sem)
    load.start()
    greet(p)
    load.wait()
    w = Wires(send_sems, recv_sems, p.cn)

    def pick(replica):
        found = jnp.int32(0)
        for r in range(p.copies):
            found = jnp.maximum(found, jnp.where(partner[r] == replica, jnp.int32(r), jnp.int32(0)))
        return found

    out, through, back = exchange(w, "e", full.at[0, me], spread, chosen, full.at[1, me], pick, p)
    own, taught = gather(w, "s", full.at[0], p), gather(w, "t", full.at[1], p)
    out()
    own[0]()
    own[1]()
    through()
    for step in own[2:12]:
        step()
    back()
    taught[0]()
    for step in own[12:-1]:
        step()
    for step in taught[1:]:
        step()
    own[-1]()
    w.drain()


def result_kernel(
    sizes, scale, partner, part, full, got_c, put_x, got_x, put_z, got_z, put_b, got_b,
    mine, taught, teacher, spread, chosen, send_sems, recv_sems,
):
    p = Place(sizes)
    me = p.block(p.z, p.x, p.c)
    greet(p)
    w = Wires(send_sems, recv_sems, p.cn)

    def keep_taught(where, value):
        taught[:, where] = value.astype(BF)

    def keep_mine(where, value):
        mine[:, where] = value

    runs = [
        scatter(w, tag, *(r.at[k] for r in (part, got_c, put_x, got_x, put_z, got_z, put_b, got_b)), p, keep)
        for tag, k, keep in (("t", 1, keep_taught), ("s", 0, keep_mine))
    ]
    out, through, back = exchange(w, "e", taught, spread, chosen, teacher, lambda r: partner[r], p)
    runs[0][0]()
    runs[1][0]()
    for step in runs[0][1:]:
        step()
    out()
    middle = len(runs[1]) // 3
    for step in runs[1][1:middle]:
        step()
    through()
    for step in runs[1][middle:]:
        step()
    back()
    full[me] = ((mine[...] - teacher[...].astype(F32)) * scale).astype(BF)
    for step in gather(w, "g", full, p):
        step()
    w.drain()


def vmem():
    return pl.BlockSpec(memory_space=pltpu.VMEM)


def params(number):
    return pltpu.CompilerParams(
        collective_id=number, has_side_effects=True, vmem_limit_bytes=60 * 1024 * 1024
    )


def fetch_tokens(sizes, partner, tokens):
    rows, width = tokens.shape
    members, copies = sizes["z"] * 4, sizes["ry"] * sizes["rx"]
    return pl.pallas_call(
        functools.partial(token_kernel, sizes),
        out_shape=jax.ShapeDtypeStruct((2, members, rows, width), BF),
        in_specs=[pl.BlockSpec(memory_space=pltpu.SMEM), pl.BlockSpec(memory_space=pl.ANY)],
        out_specs=vmem(),
        scratch_shapes=[
            pltpu.VMEM((copies, rows, width // copies), BF),
            pltpu.VMEM((copies, rows, width // copies), BF),
            pltpu.SemaphoreType.DMA,
            pltpu.SemaphoreType.DMA((256,)),
            pltpu.SemaphoreType.DMA((256,)),
        ],
        compiler_params=params(0),
        name="fetch_tokens",
    )(partner, tokens)


def cotangents(sizes, scale, partner, part):
    rows, width = part.shape[-2:]
    deep, members, copies = sizes["z"], sizes["z"] * 4, sizes["ry"] * sizes["rx"]
    half, q = deep // 2, width // 4
    return pl.pallas_call(
        functools.partial(result_kernel, sizes, scale),
        out_shape=jax.ShapeDtypeStruct((members, rows, width), BF),
        in_specs=[pl.BlockSpec(memory_space=pltpu.SMEM), vmem()],
        out_specs=vmem(),
        scratch_shapes=[
            pltpu.VMEM((2, deep, 2, rows, width), BF),
            pltpu.VMEM((2, deep, rows, 2 * q), BF),
            pltpu.VMEM((2, deep, rows, 2 * q), BF),
            pltpu.VMEM((2, 2, half, rows, 6 * q), BF),
            pltpu.VMEM((2, 2, half, rows, 6 * q), BF),
            pltpu.VMEM((2, rows, 2 * q), BF),
            pltpu.VMEM((2, rows, 2 * q), BF),
            pltpu.VMEM((rows, width), F32),
            pltpu.VMEM((rows, width), BF),
            pltpu.VMEM((rows, width), BF),
            pltpu.VMEM((copies, rows, width // copies), BF),
            pltpu.VMEM((copies, rows, width // copies), BF),
            pltpu.SemaphoreType.DMA((320,)),
            pltpu.SemaphoreType.DMA((320,)),
        ],
        compiler_params=params(1),
        name="cotangents",
    )(partner, part)


def contract(left, right, left_dim, right_dim):
    return lax.dot_general(
        left, right, (((left_dim,), (right_dim,)), ((), ())), preferred_element_type=F32
    )


def local(sizes, partner, tokens, w_gate, w_up, w_down):
    rows, width = tokens.shape[1:]
    members = sizes["z"] * 4
    count = rows * members
    scale = 1.0 / math.sqrt(count)
    full = fetch_tokens(sizes, partner, tokens[0])
    both = full.reshape(2 * count, width)
    gates = contract(w_gate[0], both, 1, 1)
    ups = contract(w_up[0], both, 1, 1)
    hiddens = (jax.nn.silu(gates) * ups).astype(BF)
    part = contract(hiddens, w_down[0], 0, 0).astype(BF)
    cot = cotangents(sizes, scale, partner, part.reshape(2, sizes["z"], 2, 2, rows, width))
    cot = cot.reshape(count, width)
    rows_all, hidden, pre_gate, pre_up = both[:count], hiddens[:, :count], gates[:, :count], ups[:, :count]
    grad_down = contract(hidden, cot, 1, 0).astype(BF)
    d_hidden = contract(w_down[0], cot, 1, 1)
    sigma = jax.nn.sigmoid(pre_gate)
    d_gate = (d_hidden * pre_up * sigma * (1.0 + pre_gate * (1.0 - sigma))).astype(BF)
    d_up = (d_hidden * pre_gate * sigma).astype(BF)
    grad_gate = contract(d_gate, rows_all, 1, 0).astype(BF)
    grad_up = contract(d_up, rows_all, 1, 0).astype(BF)
    return (grad_gate[None], grad_up[None], grad_down[None])


def solution(mesh):
    members, copies = mesh.shape["fsdp"], mesh.shape["replica"]
    sizes = {"ry": copies // 2, "rx": 2, "z": members // 4, "x": 2, "c": 2}
    split = Mesh(mesh.devices.reshape(tuple(sizes.values())), tuple(sizes))
    spec = P(REPLICA, FSDP, None)
    return jax.shard_map(
        functools.partial(local, sizes),
        mesh=split,
        in_specs=(P(), spec, spec, spec, spec),
        out_specs=(spec, spec, spec),
        check_vma=False,
    )
```

time: 422 us -> 171 us (0.41)
  waiting for transfers between devices: 285 us -> 0 us
  Pallas kernels: 0 us -> 142 us
  other arithmetic: 34.4 us -> 0 us
  blocking collectives: 18.9 us -> 0 us
  local copies, waits for them, and re-layouts: 20.5 us -> 2.35 us
  starting transfers between devices: 15.1 us -> 0 us
  between operations: 13.9 us -> 0.73 us
  matrix products: 33.6 us -> 26 us
    all_gather x2 -> x0, waiting for transfers between devices: 142 us -> none  [the longest x1 74.8 us: in_one_piece(): filled = lax.all_gather(both, axis, axis=dim, tiled=True)]
    pallas_call x0 -> x2, Pallas kernels: none -> 142 us  [the longest x1 79.9 us: cotangents(): pl.pallas_call(functools.partial(result_kernel, sizes, scale), out_shape=...]
    reduce_scatter x1 -> x0, waiting for transfers between devices: 127 us -> none  [side_by_side(): filled = lax.psum_scatter(both, axis, scatter_dimension=dim, tiled=True)]
    unnamed x3 -> x0, other arithmetic: 23.5 us -> none
    all_to_all x2 -> x0, blocking collectives: 18.9 us -> none  [the longest x1 9.44 us: local(): lax.all_to_all(row_chosen, REPLICA, split_axis=0, concat_axis=2, tiled=True)]
    all_to_all x3 -> x0, waiting for transfers between devices: 15.9 us -> none  [the longest x2 8.89 us: moved_by_axis(): filled = lax.all_to_all(filled, axes[k], k, k, tiled=True)]
    all_to_all x3 -> x0, starting transfers between devices: 15 us -> none  [the longest x2 9.01 us: moved_by_axis(): filled = lax.all_to_all(filled, axes[k], k, k, tiled=True)]
    concatenate x2 -> x0, other arithmetic: 9.32 us -> none  [the longest x1 7.69 us: side_by_side(): both = jnp.concatenate(arrays, axis=along)]
  transfers between devices with their start and end apart: 6 -> 0, of which waited for: 6 -> 0; matrix products, arithmetic and copies ran while one was open for 0% -> 0% of each run, Pallas kernels for 0% -> 0%
where the time goes in v1:
time: 171 us
  Pallas kernels  142 us (83%)
  matrix products  26 us (15%)
  local copies, waits for them, and re-layouts  2.35 us (1%)
    pallas_call x1, Pallas kernels, cotangents(): pl.pallas_call(functools.partial(result_kernel, sizes, scale), out_shape=...  79.9 us
    pallas_call x1, Pallas kernels, fetch_tokens(): pl.pallas_call(functools.partial(token_kernel, sizes), out_shape=jax.Shap...  61.7 us
    dot_general x7, matrix products, contract(): lax.dot_general(left, right, (((left_dim,), (right_dim,)), ((), ())), pre...  26 us

profile of v1, /device:TPU:1, one launch (start us, length us, event | category | flops | bytes accessed | tf_op | source)
XLA Modules:
  0.0 170.7 jit_solution(13776058578847832019)
XLA Ops:
  0.6 0.0 copy-start
  0.6 61.7 %fetch_tokens.1 = bf16[2,32,16,4096]{3,2,1,0:T(8,128)(2,1)} custom-call(s32[8]{0:T(128)} %partner.3, bf16[16,4096]{1,0:T(8,128)(2,1)} %bitcast.50), custom_call_target="tpu_custom_call" | custom-call | tf_op jit(solution)/shard_map/fetch_tokens/pallas_call | solution.py:367
  62.3 0.0 copy-start.2
  62.3 0.0 copy-start.4
  62.3 6.7 %fusion.10 = f32[224,1024]{1,0:T(8,128)S(1)} fusion(bf16[1024,4096]{1,0:T(8,128)(2,1)} %bitcast.46, bf16[1,224,4096]{2,1,0:T(8,128)(2,1)} %param.7), kind=kOutput, calls=%fused_computation.14 | convolution fusion | flops 1879048192 | bytes 11141120 | tf_op jit(solution)/shard_map/dot_general | solution.py:415
  69.0 0.0 copy-done.2
  69.1 0.1 copy-done.4
  69.1 2.7 %multiply_convert_fusion = (bf16[224,1024]{1,0:T(8,128)(2,1)S(1)}, f32[224,1024]{1,0:T(8,128)S(1)}) fusion(f32[224,1024]{1,0:T(8,128)S(1)} %fusion.10, bf16[1024,4096]{1,0:T(8,128)(2,1)S(1)} %bitcast.47, bf16[1,224,4096]{2,1,0:T(8,128)(2,1)S(1)} %copy-done.4), kind=kOutput, calls=%fused_computation.17 | convolution fusion | flops 1880424448 | bytes 12517376 | tf_op jit(solution)/shard_map/dot_general | solution.py:415
  71.8 2.2 %slice.17 = bf16[1,32,16,4096]{3,2,1,0:T(8,128)(2,1)} slice(bf16[2,32,16,4096]{3,2,1,0:T(8,128)(2,1)S(1)} %copy-done.2), slice={[0:1], [0:32], [0:16], [0:4096]} | slice | bytes 8388608 | tf_op jit(solution)/shard_map/slice | solution.py:433
  74.1 0.0 copy-done
  74.1 5.6 %convolution_convert_fusion = bf16[1024,4096]{1,0:T(8,128)(2,1)} fusion(bf16[224,1024]{1,0:T(8,128)(2,1)S(1)} %get-tuple-element.3, bf16[1,224,4096]{2,1,0:T(8,128)(2,1)S(1)} %copy-done), kind=kOutput, calls=%fused_computation | convolution fusion | flops 1883242496 | bytes 10682368 | tf_op jit(solution)/shard_map/dot_general | solution.py:415
  79.7 79.9 %cotangents.1 = bf16[32,16,4096]{2,1,0:T(8,128)(2,1)} custom-call(s32[8]{0:T(128)} %partner.3, bf16[2,8,2,2,16,4096]{5,4,3,2,1,0:T(8,128)(2,1)} %bitcast.43), custom_call_target="tpu_custom_call" | custom-call | tf_op jit(solution)/shard_map/cotangents/pallas_call | solution.py:388
  159.7 0.0 copy-start.3
  159.7 3.8 %fusion.16 = f32[224,512]{1,0:T(8,128)S(1)} fusion(bf16[512,4096]{1,0:T(8,128)(2,1)} %bitcast.48, bf16[1,224,4096]{2,1,0:T(8,128)(2,1)S(1)} %copy-done), kind=kOutput, calls=%fused_computation.16 | convolution fusion | flops 939524096 | bytes 6488064 | tf_op jit(solution)/shard_map/dot_general | solution.py:415
  163.4 0.0 copy-done.3
  163.4 0.0 copy-start.1
  163.5 2.4 %fusion.2 = bf16[1,224,4096]{2,1,0:T(8,128)(2,1)} fusion(bf16[512,4096]{1,0:T(8,128)(2,1)S(1)} %bitcast.49, bf16[224,1024]{1,0:T(8,128)(2,1)S(1)} %get-tuple-element.3), kind=kOutput, calls=%fused_computation.6 | convolution fusion | flops 940441600 | bytes 6258688 | tf_op jit(solution)/shard_map/dot_general | solution.py:415
  165.8 0.0 copy-done.1
  165.9 2.4 %fusion = bf16[1,224,4096]{2,1,0:T(8,128)(2,1)} fusion(bf16[512,4096]{1,0:T(8,128)(2,1)S(1)} %bitcast.44, f32[224,512]{1,0:T(8,128)S(1)} %fusion.16, f32[224,1024]{1,0:T(8,128)S(1)} %get-tuple-element.4, f32[224,1024]{1,0:T(8,128)S(1)} %fusion.10), kind=kOutput, calls=%fused_computation.4 | convolution fusion | flops 941588480 | bytes 7405568 | tf_op jit(solution)/shard_map/dot_general | solution.py:415
  168.3 2.4 %fusion.1 = bf16[1,224,4096]{2,1,0:T(8,128)(2,1)} fusion(bf16[512,4096]{1,0:T(8,128)(2,1)S(1)} %bitcast.45, f32[224,512]{1,0:T(8,128)S(1)} %fusion.16, f32[224,1024]{1,0:T(8,128)S(1)} %fusion.10), kind=kOutput, calls=%fused_computation.5 | convolution fusion | flops 941129728 | bytes 6946816 | tf_op jit(solution)/shard_map/dot_general | solution.py:415
Async XLA Ops:
  0.6 73.5 %copy-start = (bf16[1,224,4096]{2,1,0:T(8,128)(2,1)S(1)}, bf16[1,224,4096]{2,1,0:T(8,128)(2,1)}, u32[]{:S(2)}) copy-start(bf16[1,224,4096]{2,1,0:T(8,128)(2,1)} %param.9) | copy-start | bytes 5505028
  62.3 6.7 %copy-start.2 = (bf16[2,32,16,4096]{3,2,1,0:T(8,128)(2,1)S(1)}, bf16[2,32,16,4096]{3,2,1,0:T(8,128)(2,1)}, u32[]{:S(2)}) copy-start(bf16[2,32,16,4096]{3,2,1,0:T(8,128)(2,1)} %fetch_tokens.1) | copy-start | bytes 25165828
  62.3 6.8 %copy-start.4 = (bf16[1,224,4096]{2,1,0:T(8,128)(2,1)S(1)}, bf16[1,224,4096]{2,1,0:T(8,128)(2,1)}, u32[]{:S(2)}) copy-start(bf16[1,224,4096]{2,1,0:T(8,128)(2,1)} %param.8) | copy-start | bytes 5505028
  159.7 3.8 %copy-start.3 = (bf16[32,16,4096]{2,1,0:T(8,128)(2,1)S(1)}, bf16[32,16,4096]{2,1,0:T(8,128)(2,1)}, u32[]{:S(2)}) copy-start(bf16[32,16,4096]{2,1,0:T(8,128)(2,1)} %cotangents.1) | copy-start | bytes 12582916
  163.4 2.4 %copy-start.1 = (bf16[1,32,16,4096]{3,2,1,0:T(8,128)(2,1)S(1)}, bf16[1,32,16,4096]{3,2,1,0:T(8,128)(2,1)}, u32[]{:S(2)}) copy-start(bf16[1,32,16,4096]{3,2,1,0:T(8,128)(2,1)} %slice.17) | copy-start | bytes 12582916

commit v2 on v1

v2 whole, which is shorter than its diff:
```python
import functools
import math

import jax
import jax.numpy as jnp
from jax import lax
from jax.experimental import pallas as pl
from jax.experimental.pallas import tpu as pltpu
from jax.sharding import Mesh
from jax.sharding import PartitionSpec as P

MESH = pl.DeviceIdType.MESH
REPLICA = ("ry", "rx")
FSDP = ("z", "x", "c")
BF = jnp.bfloat16
NS, NR, LEAD = 24, 232, 22
F32 = jnp.float32


class Place:
    def __init__(self, sizes):
        self.ry, self.rx, self.z, self.x, self.c = (lax.axis_index(a) for a in REPLICA + FSDP)
        self.deep, self.wide, self.copies = sizes["z"], sizes["rx"], sizes["ry"] * sizes["rx"]
        self.half = self.deep // 2
        self.replica = self.ry * self.wide + self.rx
        self.xn = {"x": 1 - self.x}
        self.cn = {"c": 1 - self.c}
        self.zn = {"+": {"z": self.at(1)}, "-": {"z": self.at(-1)}}

    def at(self, offset):
        return lax.rem(self.z + offset + self.deep, self.deep)

    def block(self, z, x, c):
        return (z * 2 + x) * 2 + c

    def other(self, offset):
        return lax.rem(self.replica + offset, self.copies)

    def peer(self, replica):
        return {"ry": replica // self.wide, "rx": lax.rem(replica, self.wide)}


class Wires:
    def __init__(self, send_sems, recv_sems, anyone):
        self.send_sems, self.recv_sems, self.anyone = send_sems, recv_sems, anyone
        self.keys, self.groups = {}, {}

    def key(self, key):
        return self.recv_sems.at[self.keys.setdefault(key, len(self.keys))]

    def send(self, src, dst, to, key, group):
        number, total = self.groups.setdefault(group, (len(self.groups), []))
        total.append(math.prod(src.shape))
        pltpu.make_async_remote_copy(
            src_ref=src,
            dst_ref=dst,
            send_sem=self.send_sems.at[number],
            recv_sem=self.key(key),
            device_id=to,
            device_id_type=MESH,
        ).start()

    def of(self, ref, semaphore):
        return pltpu.make_async_remote_copy(
            src_ref=ref,
            dst_ref=ref,
            send_sem=semaphore,
            recv_sem=semaphore,
            device_id=self.anyone,
            device_id_type=MESH,
        )

    def wait(self, ref, key):
        self.of(ref, self.key(key)).wait_recv()

    def drain(self, sized):
        for number, total in self.groups.values():
            self.of(sized(sum(total)), self.send_sems.at[number]).wait_send()


def greet(p):
    barrier = pltpu.get_barrier_semaphore()
    friends = [p.xn, p.cn, p.zn["+"], p.zn["-"]]
    friends += [p.peer(p.other(o)) for o in range(1, p.copies)]
    for friend in friends:
        pl.semaphore_signal(barrier, inc=1, device_id=friend, device_id_type=MESH)
    pl.semaphore_wait(barrier, len(friends))


def hops_of(half):
    reach = {}
    for name in ("a1", "o"):
        reach["+", name], reach["-", name] = half, half - 1
    for name in ("a2", "t"):
        reach["+", name], reach["-", name] = half - 1, half
    return reach


NAMES = ("a1", "a2", "o", "t")


def gather(w, tag, full, p):
    q = full.shape[-1] // 4
    cols = {"a1": pl.ds(0, q), "a2": pl.ds(q, q), "o": pl.ds(2 * q, 2 * q), "t": pl.ds(2 * q, 2 * q)}
    reach = hops_of(p.half)
    whole = pl.ds(0, 4 * q)
    steps = []

    def piece(z, x, c, name):
        return full.at[p.block(z, x, c), :, whole if name == "all" else cols[name]]

    def put(z, x, name, to, key):
        ref = piece(z, x, p.c, name)
        w.send(ref, ref, to, key, (tag, "z" + key[1] if to is p.zn["+"] or to is p.zn["-"] else "x"))

    def share(z, x, name):
        ref = piece(z, x, p.c, name)
        w.send(ref, ref, p.cn, (tag, "c"), (tag, "c"))

    def own():
        put(p.z, p.x, "o", p.xn, (tag, "xb"))
        for name in ("a1", "a2", "o"):
            for way in "+-":
                put(p.z, p.x, name, p.zn[way], (tag, way, 1, name))
        for name in ("a1", "a2"):
            put(p.z, p.x, name, p.xn, (tag, "xa", "+", 0, name))
        share(p.z, p.x, "all")

    def crossed():
        w.wait(piece(p.z, 1 - p.x, p.c, "t"), (tag, "xb"))
        for way in "+-":
            put(p.z, 1 - p.x, "t", p.zn[way], (tag, way, 1, "t"))
        share(p.z, 1 - p.x, "t")

    def from_x(way, s, name):
        z = p.at(-s if way == "+" else s)
        w.wait(piece(z, 1 - p.x, p.c, name), (tag, "xa", way, s, name))
        share(z, 1 - p.x, name)

    def from_z(way, s, name):
        z = p.at(-s if way == "+" else s)
        x = 1 - p.x if name == "t" else p.x
        w.wait(piece(z, x, p.c, name), (tag, way, s, name))
        if s < reach[way, name]:
            put(z, x, name, p.zn[way], (tag, way, s + 1, name))
        if name in ("a1", "a2"):
            put(z, x, name, p.xn, (tag, "xa", way, s, name))
        share(z, x, name)

    def last():
        w.wait(full.at[pl.ds(0, 2 * p.deep)], (tag, "c"))

    steps += [own, crossed]
    steps += [functools.partial(from_x, "+", 0, name) for name in ("a1", "a2")]
    for s in range(1, p.half + 1):
        for name in NAMES:
            for way in "+-":
                if s <= reach[way, name]:
                    steps.append(functools.partial(from_z, way, s, name))
        for name in ("a1", "a2"):
            for way in "+-":
                if 1 <= s - 1 <= reach[way, name]:
                    steps.append(functools.partial(from_x, way, s - 1, name))
    for name in ("a1", "a2"):
        for way in "+-":
            if p.half <= reach[way, name]:
                steps.append(functools.partial(from_x, way, p.half, name))
    steps.append(last)
    return steps


def exchange(w, tag, src, spread, chosen, dst, pick, p):
    width = src.shape[-1] // p.copies

    def chunk(k):
        return pl.ds(pl.multiple_of(k * width, width), width)

    def out():
        for o in range(1, p.copies):
            k = p.other(o)
            w.send(src.at[:, chunk(k)], spread.at[p.replica], p.peer(k), (tag, "out"), (tag, "out"))
        spread[p.replica] = src[:, chunk(p.replica)]

    def through():
        w.wait(spread.at[pl.ds(0, p.copies - 1)], (tag, "out"))
        for o in range(1, p.copies):
            r = p.other(o)
            chosen[o] = spread[pick(r)]
            w.send(chosen.at[o], dst.at[:, chunk(p.replica)], p.peer(r), (tag, "back"), (tag, "back"))
        dst[:, chunk(p.replica)] = spread[pick(p.replica)]

    def back():
        w.wait(dst.at[:, pl.ds(0, (p.copies - 1) * width)], (tag, "back"))

    return [out, through, back]


def scatter(w, tag, part, got_c, put_x, got_x, put_z, got_z, put_b, got_b, p, finish):
    q = part.shape[-1] // 4
    a = pl.ds(0, 2 * q)
    cols = {"a1": pl.ds(0, q), "a2": pl.ds(q, q), "o": pl.ds(2 * q, 2 * q), "t": pl.ds(2 * q, 2 * q)}
    slot = {"a1": pl.ds(0, q), "a2": pl.ds(q, q), "o": pl.ds(2 * q, 2 * q), "t": pl.ds(4 * q, 2 * q)}
    reach = hops_of(p.half)
    index = {"+": 0, "-": 1}
    steps = []
    seen = set()

    def pair(z, x, where):
        return part[z, x, p.c, :, where].astype(F32) + got_c[z, x, :, where].astype(F32)

    def offsets(d):
        return (0,) if d == 0 else ((d,) if d == p.half else (d, -d))

    def halves():
        for d in range(p.half, -1, -1):
            for o in offsets(d):
                z = p.at(o)
                w.send(part.at[z, :, 1 - p.c], got_c.at[z], p.cn, (tag, "c", o), (tag, "c"))

    def cross(o):
        z = p.at(o)
        w.wait(got_c.at[z], (tag, "c", o))
        put_x[z] = pair(z, 1 - p.x, a).astype(BF)
        w.send(put_x.at[z], got_x.at[z], p.xn, (tag, "x", o), (tag, "x"))

    def value(z, name, where):
        x = 1 - p.x if name == "t" else p.x
        total = pair(z, x, where)
        if name in ("a1", "a2"):
            total += got_x[z, :, where].astype(F32)
        return total

    def arrived(o, name):
        if name in ("a1", "a2") and o not in seen:
            seen.add(o)
            w.wait(got_x.at[p.at(o)], (tag, "x", o))

    def came(way, d, name):
        ref = got_z.at[index[way], d - 1, :, slot[name]]
        w.wait(ref, (tag, way, d, name))
        return ref[...].astype(F32)

    def onward(way, d, name):
        o = d if way == "+" else (p.half if d == p.half else -d)
        z = p.at(o)
        arrived(o, name)
        total = value(z, name, cols[name])
        if d < reach[way, name]:
            total += came(way, d + 1, name)
        ref = put_z.at[index[way], d - 1, :, slot[name]]
        ref[...] = total.astype(BF)
        w.send(ref, got_z.at[index[way], d - 1, :, slot[name]], p.zn[way], (tag, way, d, name), (tag, "z" + way))

    def ended(name):
        arrived(0, name)
        total = value(p.z, name, cols[name])
        for way in "+-":
            if 1 <= reach[way, name]:
                total += came(way, 1, name)
        return total

    def hand():
        put_b[...] = ended("t").astype(BF)
        w.send(put_b, got_b, p.xn, (tag, "b"), (tag, "x"))
        finish(cols["a1"], ended("a1"))
        finish(cols["a2"], ended("a2"))

    def last():
        total = ended("o")
        w.wait(got_b, (tag, "b"))
        finish(cols["o"], total + got_b[...].astype(F32))

    def outward(d, names, fresh):
        return [
            functools.partial(onward, way, d, name)
            for name in names
            for way in "+-"
            if (d == reach[way, name] if fresh else d < reach[way, name])
        ]

    def crosses(d):
        return [functools.partial(cross, o) for o in offsets(d)] if d >= 0 else []

    top = p.half
    steps += [halves] + crosses(top) + outward(top, ("o", "t"), True)
    steps += crosses(top - 1) + outward(top - 1, ("o", "t"), True) + crosses(top - 2)
    steps += outward(top, ("a1", "a2"), True) + outward(top - 1, ("a1", "a2"), True)
    for d in range(top - 1, 0, -1):
        steps += outward(d, ("a1", "a2"), False) + crosses(d - 2) + outward(d, ("o", "t"), False)
    steps += [hand, last]
    return steps


def contract(left, right, left_dim, right_dim):
    return lax.dot_general(
        left, right, (((left_dim,), (right_dim,)), ((), ())), preferred_element_type=F32
    )


def mixed(steps, work):
    done = 0
    for k, step in enumerate(steps):
        step()
        while done < len(work) * (k + 1) // len(steps):
            work[done]()
            done += 1
    for piece in work[done:]:
        piece()


def forward(rows, pre, hidden, part, both_t, w_down):
    members, high, width = rows.shape
    q, units, lane = width // 4, hidden.shape[1], pre.shape[1] // 2
    count = members * high

    def grow(k):
        where = pl.ds(k * q, q)
        product = contract(rows[:, :, where].reshape(count, q), both_t[where, :], 1, 0)
        pre[...] = product if k == 0 else pre[...] + product

    def activate():
        gate = pre[:, pl.ds(0, units)]
        hidden[...] = (gate * jax.nn.sigmoid(gate) * pre[:, pl.ds(lane, units)]).astype(BF)

    def lower(k):
        where = pl.ds(k * q, q)
        product = contract(hidden[...], w_down[:, where], 1, 0).astype(BF)
        part[..., where] = product.reshape(part.shape[:-1] + (q,))

    work = [functools.partial(grow, k) for k in range(4)]
    return work + [activate] + [functools.partial(lower, k) for k in range(4)]


def kernel(sizes, scale, *refs):
    (
        partner, tokens, gate_in, up_in, down_in,
        rows_out, cot_out, hidden, d_gate, d_up,
        full, cot, w_gate, w_up, w_down, both_t, down_t, pre, far_pre, far_hidden,
        part, got_c, put_x, got_x, put_z, got_z, put_b, got_b,
        mine, taught, teacher, spread, chosen, spread_back, chosen_back, load_sems, send_sems, recv_sems,
    ) = refs
    p = Place(sizes)
    me = p.block(p.z, p.x, p.c)
    q = full.shape[-1] // 4
    load = pltpu.make_async_copy(tokens, full.at[me], load_sems.at[0])
    load.start()
    weights = [
        pltpu.make_async_copy(src, dst, load_sems.at[1 + k])
        for k, (src, dst) in enumerate(((gate_in, w_gate), (up_in, w_up), (down_in, w_down)))
    ]
    for copy in weights:
        copy.start()
    greet(p)
    load.wait()
    w = Wires(send_sems, recv_sems, p.cn)

    def taught_by(replica):
        found = jnp.int32(0)
        for r in range(p.copies):
            found = jnp.maximum(found, jnp.where(partner[r] == replica, jnp.int32(r), jnp.int32(0)))
        return found

    def keep_taught(where, value):
        taught[:, where] = value.astype(BF)

    def keep_mine(where, value):
        mine[:, where] = value

    rows_near, rows_far = (full.at[pl.ds(k * 4 * p.deep, 4 * p.deep)] for k in range(2))
    out, through, back = exchange(
        w, "e", rows_near.at[me], spread, chosen, rows_far.at[me], taught_by, p
    )
    near, far = gather(w, "s", rows_near, p), gather(w, "t", rows_far, p)
    near_work = forward(rows_near, pre, hidden, part.at[0], both_t, w_down)
    far_work = forward(rows_far, far_pre, far_hidden, part.at[1], both_t, w_down)
    near_sum, far_sum = (
        scatter(w, tag, *(r.at[k] for r in (part, got_c, put_x, got_x, put_z, got_z, put_b, got_b)), p, keep)
        for tag, k, keep in (("a", 0, keep_mine), ("b", 1, keep_taught))
    )
    back_out, back_through, back_back = exchange(
        w, "f", taught, spread_back, chosen_back, teacher, lambda r: partner[r], p
    )

    units, lane = hidden.shape[1], pre.shape[1] // 2

    def turn(src, dst, start, k):
        where = pl.ds(k * q, q)
        dst[where, pl.ds(start, units)] = src[:, where].T
        if dst is both_t and lane > units:
            dst[where, pl.ds(start + units, lane - units)] = jnp.zeros((q, lane - units), BF)

    turns = [
        functools.partial(turn, src, dst, start, k)
        for src, dst, start in ((w_gate, both_t, 0), (w_up, both_t, lane), (w_down, down_t, 0))
        for k in range(4)
    ]
    near[0]()
    out()
    for copy in weights:
        copy.wait()
    mixed(near[1:12], turns)
    through()
    mixed(near[12:24], [])
    back()
    far[0]()
    mixed(near[24:34], [])
    mixed(far[1:4], [])
    mixed(near[34:-1], far[4:12])
    near[-1]()
    keep_rows = pltpu.make_async_copy(rows_near, rows_out, load_sems.at[4])
    keep_rows.start()
    mixed(far[12:], near_work)
    near_sum[0]()
    mixed(far_work, near_sum[1:9])
    far_sum[0]()
    mixed(far_sum[1:9], [])
    mixed(far_sum[9:], near_sum[9:LEAD])
    back_out()
    mixed(near_sum[LEAD:-6], [])
    back_through()
    mixed(near_sum[-6:], [])
    back_back()
    cot[me] = ((mine[...] - teacher[...].astype(F32)) * scale).astype(BF)
    mixed(gather(w, "g", cot, p), [])
    keep_cot = pltpu.make_async_copy(cot, cot_out, load_sems.at[5])
    keep_cot.start()
    count = pre.shape[0]

    def pull(k):
        where = pl.ds(k * q, q)
        product = contract(cot[:, :, where].reshape(count, q), down_t[where, :], 1, 0)
        here = pl.ds(0, units)
        far_pre[:, here] = product if k == 0 else far_pre[:, here] + product

    for k in range(4):
        pull(k)
    gate, up, d_hidden = pre[:, pl.ds(0, units)], pre[:, pl.ds(lane, units)], far_pre[:, pl.ds(0, units)]
    sigma = jax.nn.sigmoid(gate)
    d_gate[...] = (d_hidden * up * sigma * (1.0 + gate * (1.0 - sigma))).astype(BF)
    d_up[...] = (d_hidden * gate * sigma).astype(BF)
    keep_cot.wait()

    def sized(elements):
        unit = full.shape[1] * q
        if elements % unit:
            return chosen.at[pl.ds(0, p.copies - 1)]
        return full.at[pl.ds(0, elements // unit), :, pl.ds(0, q)]

    keep_rows.wait()
    w.drain(sized)


def fused(sizes, scale, partner, tokens, w_gate, w_up, w_down):
    rows, width = tokens.shape
    units = w_gate.shape[0]
    lane = pl.cdiv(units, 128) * 128
    deep, members, copies = sizes["z"], sizes["z"] * 4, sizes["ry"] * sizes["rx"]
    half, q, count = deep // 2, width // 4, rows * members
    anywhere, vmem = pl.BlockSpec(memory_space=pl.ANY), pl.BlockSpec(memory_space=pltpu.VMEM)
    chunk = pltpu.VMEM((copies, rows, width // copies), BF)
    return pl.pallas_call(
        functools.partial(kernel, sizes, scale),
        out_shape=[
            jax.ShapeDtypeStruct((members, rows, width), BF),
            jax.ShapeDtypeStruct((members, rows, width), BF),
            jax.ShapeDtypeStruct((count, units), BF),
            jax.ShapeDtypeStruct((count, units), BF),
            jax.ShapeDtypeStruct((count, units), BF),
        ],
        in_specs=[pl.BlockSpec(memory_space=pltpu.SMEM)] + [anywhere] * 4,
        out_specs=[anywhere] * 2 + [vmem] * 3,
        scratch_shapes=[
            pltpu.VMEM((2 * members, rows, width), BF),
            pltpu.VMEM((members, rows, width), BF),
            pltpu.VMEM((units, width), BF),
            pltpu.VMEM((units, width), BF),
            pltpu.VMEM((units, width), BF),
            pltpu.VMEM((width, 2 * lane), BF),
            pltpu.VMEM((width, units), BF),
            pltpu.VMEM((count, 2 * lane), F32),
            pltpu.VMEM((count, 2 * lane), F32),
            pltpu.VMEM((count, units), BF),
            pltpu.VMEM((2, deep, 2, 2, rows, width), BF),
            pltpu.VMEM((2, deep, 2, rows, width), BF),
            pltpu.VMEM((2, deep, rows, 2 * q), BF),
            pltpu.VMEM((2, deep, rows, 2 * q), BF),
            pltpu.VMEM((2, 2, half, rows, 6 * q), BF),
            pltpu.VMEM((2, 2, half, rows, 6 * q), BF),
            pltpu.VMEM((2, rows, 2 * q), BF),
            pltpu.VMEM((2, rows, 2 * q), BF),
            pltpu.VMEM((rows, width), F32),
            pltpu.VMEM((rows, width), BF),
            pltpu.VMEM((rows, width), BF),
            chunk,
            chunk,
            chunk,
            chunk,
            pltpu.SemaphoreType.DMA((6,)),
            pltpu.SemaphoreType.DMA((NS,)),
            pltpu.SemaphoreType.DMA((NR,)),
        ],
        compiler_params=pltpu.CompilerParams(
            collective_id=0, has_side_effects=True, vmem_limit_bytes=62 * 1024 * 1024
        ),
        name="step",
    )(partner, tokens, w_gate, w_up, w_down)


def local(sizes, partner, tokens, w_gate, w_up, w_down):
    rows, width = tokens.shape[1:]
    count = rows * sizes["z"] * 4
    scale = 1.0 / math.sqrt(count)
    rows_all, cot, hidden, d_gate, d_up = fused(
        sizes, scale, partner, tokens[0], w_gate[0], w_up[0], w_down[0]
    )
    rows_all, cot = rows_all.reshape(count, width), cot.reshape(count, width)
    grad_down = contract(hidden, cot, 0, 0).astype(BF)
    grad_gate = contract(d_gate, rows_all, 0, 0).astype(BF)
    grad_up = contract(d_up, rows_all, 0, 0).astype(BF)
    return (grad_gate[None], grad_up[None], grad_down[None])


def solution(mesh):
    members, copies = mesh.shape["fsdp"], mesh.shape["replica"]
    sizes = {"ry": copies // 2, "rx": 2, "z": members // 4, "x": 2, "c": 2}
    split = Mesh(mesh.devices.reshape(tuple(sizes.values())), tuple(sizes))
    spec = P(REPLICA, FSDP, None)
    return jax.shard_map(
        functools.partial(local, sizes),
        mesh=split,
        in_specs=(P(), spec, spec, spec, spec),
        out_specs=(spec, spec, spec),
        check_vma=False,
    )
```

time: 171 us -> 133 us (0.78)
  Pallas kernels: 142 us -> 123 us
  matrix products: 26 us -> 9.57 us
  local copies, waits for them, and re-layouts: 2.35 us -> 0.17 us
    pallas_call x2 -> x1, Pallas kernels: 142 us -> 123 us  [fused(): pl.pallas_call(functools.partial(kernel, sizes, scale), out_shape=[jax.Sh...]
    dot_general x7 -> x3, matrix products: 26 us -> 9.57 us  [contract(): lax.dot_general(left, right, (((left_dim,), (right_dim,)), ((), ())), pre...]
    slice x1 -> x0, local copies, waits for them, and re-layouts: 2.23 us -> none  [local(): both[:count]]
where the time goes in v2:
time: 133 us
  Pallas kernels  123 us (92%)
  matrix products  9.57 us (7%)
    pallas_call x1, Pallas kernels, fused(): pl.pallas_call(functools.partial(kernel, sizes, scale), out_shape=[jax.Sh...  123 us
    dot_general x3, matrix products, contract(): lax.dot_general(left, right, (((left_dim,), (right_dim,)), ((), ())), pre...  9.57 us

profile of v2, /device:TPU:1, one launch (start us, length us, event | category | flops | bytes accessed | tf_op | source)
XLA Modules:
  0.0 133.2 jit_solution(14340936556038725489)
XLA Ops:
  0.6 122.7 %step.1 = (bf16[32,16,4096]{2,1,0:T(8,128)(2,1)}, bf16[32,16,4096]{2,1,0:T(8,128)(2,1)}, bf16[512,224]{1,0:T(8,128)(2,1)}, bf16[512,224]{1,0:T(8,128)(2,1)}, bf16[512,224]{1,0:T(8,128)(2,1)}) custom-call(s32[8]{0:T(128)} %refs_0_.1, bf16[16,4096]{1,0:T(8,128)(2,1)} %bitcast.24, bf16[224,4096]{1,0:T(8,128)(2,1)} %bitcast.21, bf16[224,4096]{1,0:T(8,128)(2,1)} %bitcast.22, ...), custom_call_target="tpu_custom_call" | custom-call | tf_op jit(solution)/shard_map/step/pallas_call | solution.py:461
  123.4 0.0 copy-start
  123.4 0.0 copy-start.3
  123.4 4.8 %fusion.1 = bf16[1,224,4096]{2,1,0:T(8,128)(2,1)} fusion(bf16[512,224]{1,0:T(8,128)(2,1)} %get-tuple-element.10, bf16[512,4096]{1,0:T(8,128)(2,1)} %bitcast.18), kind=kOutput, calls=%fused_computation.4 | convolution fusion | flops 940441600 | bytes 6258688 | tf_op jit(solution)/shard_map/dot_general | solution.py:295
  128.2 0.0 copy-done
  128.2 0.0 copy-done.3
  128.2 0.0 copy-start.1
  128.2 0.0 copy-start.2
  128.2 2.4 %fusion = bf16[1,224,4096]{2,1,0:T(8,128)(2,1)} fusion(bf16[512,224]{1,0:T(8,128)(2,1)S(1)} %copy-done.3, bf16[512,4096]{1,0:T(8,128)(2,1)S(1)} %bitcast.19), kind=kOutput, calls=%fused_computation.3 | convolution fusion | flops 940441600 | bytes 6258688 | tf_op jit(solution)/shard_map/dot_general | solution.py:295
  130.6 0.0 copy-done.1
  130.6 0.2 copy-done.2
  130.8 2.4 %fusion.2 = bf16[1,224,4096]{2,1,0:T(8,128)(2,1)} fusion(bf16[512,224]{1,0:T(8,128)(2,1)S(1)} %copy-done.2, bf16[512,4096]{1,0:T(8,128)(2,1)S(1)} %bitcast.20), kind=kOutput, calls=%fused_computation.5 | convolution fusion | flops 940441600 | bytes 6258688 | tf_op jit(solution)/shard_map/dot_general | solution.py:295
Async XLA Ops:
  123.4 4.8 %copy-start = (bf16[32,16,4096]{2,1,0:T(8,128)(2,1)S(1)}, bf16[32,16,4096]{2,1,0:T(8,128)(2,1)}, u32[]{:S(2)}) copy-start(bf16[32,16,4096]{2,1,0:T(8,128)(2,1)} %get-tuple-element.9) | copy-start | bytes 12582916
  123.4 4.8 %copy-start.3 = (bf16[512,224]{1,0:T(8,128)(2,1)S(1)}, bf16[512,224]{1,0:T(8,128)(2,1)}, u32[]{:S(2)}) copy-start(bf16[512,224]{1,0:T(8,128)(2,1)} %get-tuple-element.8) | copy-start | bytes 688132
  128.2 2.4 %copy-start.1 = (bf16[32,16,4096]{2,1,0:T(8,128)(2,1)S(1)}, bf16[32,16,4096]{2,1,0:T(8,128)(2,1)}, u32[]{:S(2)}) copy-start(bf16[32,16,4096]{2,1,0:T(8,128)(2,1)} %get-tuple-element.12) | copy-start | bytes 12582916
  128.2 2.6 %copy-start.2 = (bf16[512,224]{1,0:T(8,128)(2,1)S(1)}, bf16[512,224]{1,0:T(8,128)(2,1)}, u32[]{:S(2)}) copy-start(bf16[512,224]{1,0:T(8,128)(2,1)} %get-tuple-element.11) | copy-start | bytes 688132

commit v3 on v2

--- a/solution.py
+++ b/solution.py
@@ -13,7 +13,7 @@
 REPLICA = ("ry", "rx")
 FSDP = ("z", "x", "c")
 BF = jnp.bfloat16
-NS, NR, LEAD = 24, 232, 22
+NS, NR, EARLY, LEAD, LATE, PARTS = 24, 232, 7, 21, 4, 2
 F32 = jnp.float32
 
 
@@ -282,11 +282,11 @@
         return [functools.partial(cross, o) for o in offsets(d)] if d >= 0 else []
 
     top = p.half
-    steps += [halves] + crosses(top) + outward(top, ("o", "t"), True)
-    steps += crosses(top - 1) + outward(top - 1, ("o", "t"), True) + crosses(top - 2)
+    steps += [halves] + crosses(top) + outward(top, ("t", "o"), True)
+    steps += crosses(top - 1) + outward(top - 1, ("t", "o"), True) + crosses(top - 2)
     steps += outward(top, ("a1", "a2"), True) + outward(top - 1, ("a1", "a2"), True)
     for d in range(top - 1, 0, -1):
-        steps += outward(d, ("a1", "a2"), False) + crosses(d - 2) + outward(d, ("o", "t"), False)
+        steps += outward(d, ("t", "a1", "a2"), False) + crosses(d - 2) + outward(d, ("o",), False)
     steps += [hand, last]
     return steps
 
@@ -334,8 +334,8 @@
 def kernel(sizes, scale, *refs):
     (
         partner, tokens, gate_in, up_in, down_in,
-        rows_out, cot_out, hidden, d_gate, d_up,
-        full, cot, w_gate, w_up, w_down, both_t, down_t, pre, far_pre, far_hidden,
+        rows_out, cot_out, hidden_t, d_both_t,
+        full, cot, w_gate, w_up, w_down, both_t, pre, far_pre, hidden, far_hidden, slope_gate, slope_up, d_hidden,
         part, got_c, put_x, got_x, put_z, got_z, put_b, got_b,
         mine, taught, teacher, spread, chosen, spread_back, chosen_back, load_sems, send_sems, recv_sems,
     ) = refs
@@ -386,19 +386,20 @@
     def turn(src, dst, start, k):
         where = pl.ds(k * q, q)
         dst[where, pl.ds(start, units)] = src[:, where].T
-        if dst is both_t and lane > units:
+        if lane > units:
             dst[where, pl.ds(start + units, lane - units)] = jnp.zeros((q, lane - units), BF)
 
     turns = [
         functools.partial(turn, src, dst, start, k)
-        for src, dst, start in ((w_gate, both_t, 0), (w_up, both_t, lane), (w_down, down_t, 0))
+        for src, dst, start in ((w_gate, both_t, 0), (w_up, both_t, lane))
         for k in range(4)
     ]
     near[0]()
     out()
     for copy in weights:
         copy.wait()
-    mixed(near[1:12], turns)
+    mixed(turns, [])
+    mixed(near[1:12], [])
     through()
     mixed(near[12:24], [])
     back()
@@ -411,33 +412,42 @@
     keep_rows.start()
     mixed(far[12:], near_work)
     near_sum[0]()
-    mixed(far_work, near_sum[1:9])
+    mixed(far_work, near_sum[1:EARLY])
     far_sum[0]()
     mixed(far_sum[1:9], [])
-    mixed(far_sum[9:], near_sum[9:LEAD])
+    mixed(far_sum[9:-2], near_sum[EARLY:LEAD])
+    far_sum[-2]()
+    mixed(near_sum[LEAD : LEAD + 3], [])
+    far_sum[-1]()
     back_out()
-    mixed(near_sum[LEAD:-6], [])
+    mixed(near_sum[LEAD + 3 : -LATE], [])
     back_through()
-    mixed(near_sum[-6:], [])
+    mixed(near_sum[-LATE:], [])
     back_back()
     cot[me] = ((mine[...] - teacher[...].astype(F32)) * scale).astype(BF)
-    mixed(gather(w, "g", cot, p), [])
+    count = pre.shape[0]
+
+    def derive(k):
+        here = pl.ds(k * 128, 128)
+        gate, up = pre[here, pl.ds(0, units)], pre[here, pl.ds(lane, units)]
+        sigma = jax.nn.sigmoid(gate)
+        slope_gate[:, here] = (up * sigma * (1.0 + gate * (1.0 - sigma))).T
+        slope_up[:, here] = (gate * sigma).T
+        hidden_t[:, here] = hidden[here, :].T
+
+    last = gather(w, "g", cot, p)
+    last[0]()
+    for k in range(count // 128):
+        derive(k)
+    mixed(last[1:], [])
     keep_cot = pltpu.make_async_copy(cot, cot_out, load_sems.at[5])
     keep_cot.start()
-    count = pre.shape[0]
-
-    def pull(k):
+    for k in range(4):
         where = pl.ds(k * q, q)
-        product = contract(cot[:, :, where].reshape(count, q), down_t[where, :], 1, 0)
-        here = pl.ds(0, units)
-        far_pre[:, here] = product if k == 0 else far_pre[:, here] + product
-
-    for k in range(4):
-        pull(k)
-    gate, up, d_hidden = pre[:, pl.ds(0, units)], pre[:, pl.ds(lane, units)], far_pre[:, pl.ds(0, units)]
-    sigma = jax.nn.sigmoid(gate)
-    d_gate[...] = (d_hidden * up * sigma * (1.0 + gate * (1.0 - sigma))).astype(BF)
-    d_up[...] = (d_hidden * gate * sigma).astype(BF)
+        product = contract(w_down[:, where], cot[:, :, where].reshape(count, q), 1, 1)
+        d_hidden[...] = product if k == 0 else d_hidden[...] + product
+    d_both_t[pl.ds(0, units), :] = (d_hidden[...] * slope_gate[...]).astype(BF)
+    d_both_t[pl.ds(units, units), :] = (d_hidden[...] * slope_up[...]).astype(BF)
     keep_cot.wait()
 
     def sized(elements):
@@ -463,12 +473,11 @@
         out_shape=[
             jax.ShapeDtypeStruct((members, rows, width), BF),
             jax.ShapeDtypeStruct((members, rows, width), BF),
-            jax.ShapeDtypeStruct((count, units), BF),
-            jax.ShapeDtypeStruct((count, units), BF),
-            jax.ShapeDtypeStruct((count, units), BF),
+            jax.ShapeDtypeStruct((units, count), BF),
+            jax.ShapeDtypeStruct((2 * units, count), BF),
         ],
         in_specs=[pl.BlockSpec(memory_space=pltpu.SMEM)] + [anywhere] * 4,
-        out_specs=[anywhere] * 2 + [vmem] * 3,
+        out_specs=[anywhere] * 2 + [vmem] * 2,
         scratch_shapes=[
             pltpu.VMEM((2 * members, rows, width), BF),
             pltpu.VMEM((members, rows, width), BF),
@@ -476,10 +485,13 @@
             pltpu.VMEM((units, width), BF),
             pltpu.VMEM((units, width), BF),
             pltpu.VMEM((width, 2 * lane), BF),
-            pltpu.VMEM((width, units), BF),
             pltpu.VMEM((count, 2 * lane), F32),
             pltpu.VMEM((count, 2 * lane), F32),
             pltpu.VMEM((count, units), BF),
+            pltpu.VMEM((count, units), BF),
+            pltpu.VMEM((units, count), F32),
+            pltpu.VMEM((units, count), F32),
+            pltpu.VMEM((units, count), F32),
             pltpu.VMEM((2, deep, 2, 2, rows, width), BF),
             pltpu.VMEM((2, deep, 2, rows, width), BF),
             pltpu.VMEM((2, deep, rows, 2 * q), BF),
@@ -506,18 +518,43 @@
     )(partner, tokens, w_gate, w_up, w_down)
 
 
+def products_kernel(hidden_t, d_both_t, rows, cot, grad_gate, grad_up, grad_down):
+    units = hidden_t.shape[0]
+    both = contract(d_both_t[...], rows[...], 1, 0).astype(BF)
+    grad_gate[...] = both[:units]
+    grad_up[...] = both[units:]
+    grad_down[...] = contract(hidden_t[...], cot[...], 1, 0).astype(BF)
+
+
+def products(hidden_t, d_both_t, rows, cot):
+    (units, count), width = hidden_t.shape, rows.shape[1]
+    step = width // PARTS
+    columns = pl.BlockSpec((count, step), lambda j: (0, j))
+    return pl.pallas_call(
+        products_kernel,
+        grid=(PARTS,),
+        out_shape=[jax.ShapeDtypeStruct((units, width), BF)] * 3,
+        in_specs=[
+            pl.BlockSpec((units, count), lambda j: (0, 0)),
+            pl.BlockSpec((2 * units, count), lambda j: (0, 0)),
+            columns,
+            columns,
+        ],
+        out_specs=[pl.BlockSpec((units, step), lambda j: (0, j))] * 3,
+        compiler_params=pltpu.CompilerParams(dimension_semantics=("arbitrary",)),
+        name="products",
+    )(hidden_t, d_both_t, rows, cot)
+
+
 def local(sizes, partner, tokens, w_gate, w_up, w_down):
     rows, width = tokens.shape[1:]
     count = rows * sizes["z"] * 4
     scale = 1.0 / math.sqrt(count)
-    rows_all, cot, hidden, d_gate, d_up = fused(
+    rows_all, cot, hidden_t, d_both_t = fused(
         sizes, scale, partner, tokens[0], w_gate[0], w_up[0], w_down[0]
     )
-    rows_all, cot = rows_all.reshape(count, width), cot.reshape(count, width)
-    grad_down = contract(hidden, cot, 0, 0).astype(BF)
-    grad_gate = contract(d_gate, rows_all, 0, 0).astype(BF)
-    grad_up = contract(d_up, rows_all, 0, 0).astype(BF)
-    return (grad_gate[None], grad_up[None], grad_down[None])
+    grads = products(hidden_t, d_both_t, rows_all.reshape(count, width), cot.reshape(count, width))
+    return tuple(grad[None] for grad in grads)
 
 
 def solution(mesh):

time: 133 us -> 123 us (0.925)
  matrix products: 9.57 us -> 0 us
    dot_general x3 -> x0, matrix products: 9.57 us -> none  [contract(): lax.dot_general(left, right, (((left_dim,), (right_dim,)), ((), ())), pre...]
    pallas_call x1, Pallas kernels: 123 us -> 116 us  [fused(): pl.pallas_call(functools.partial(kernel, sizes, scale), out_shape=[jax.Sh...]
    pallas_call x0 -> x1, Pallas kernels: none -> 6.59 us  [products(): pl.pallas_call(products_kernel, grid=(PARTS,), out_shape=[jax.ShapeDtypeS...]
where the time goes in v3:
time: 123 us
  Pallas kernels  122 us (99%)
    pallas_call x1, Pallas kernels, fused(): pl.pallas_call(functools.partial(kernel, sizes, scale), out_shape=[jax.Sh...  116 us
    pallas_call x1, Pallas kernels, products(): pl.pallas_call(products_kernel, grid=(PARTS,), out_shape=[jax.ShapeDtypeS...  6.59 us

profile of v3, /device:TPU:1, one launch (start us, length us, event | category | flops | bytes accessed | tf_op | source)
XLA Modules:
  0.0 123.1 jit_solution(4871583242958960137)
XLA Ops:
  0.6 115.8 %step.1 = (bf16[32,16,4096]{2,1,0:T(8,128)(2,1)}, bf16[32,16,4096]{2,1,0:T(8,128)(2,1)}, bf16[224,512]{1,0:T(8,128)(2,1)}, bf16[448,512]{1,0:T(8,128)(2,1)}) custom-call(s32[8]{0:T(128)} %refs_0_.1, bf16[16,4096]{1,0:T(8,128)(2,1)} %bitcast.14, bf16[224,4096]{1,0:T(8,128)(2,1)} %bitcast.11, bf16[224,4096]{1,0:T(8,128)(2,1)} %bitcast.12, ...), custom_call_target="tpu_custom_call" | custom-call | tf_op jit(solution)/shard_map/step/pallas_call | solution.py:471
  116.5 6.6 %products.1 = (bf16[224,4096]{1,0:T(8,128)(2,1)}, bf16[224,4096]{1,0:T(8,128)(2,1)}, bf16[224,4096]{1,0:T(8,128)(2,1)}) custom-call(bf16[224,512]{1,0:T(8,128)(2,1)} %get-tuple-element.10.hidden_t, bf16[448,512]{1,0:T(8,128)(2,1)} %get-tuple-element.11.d_both_t, bf16[512,4096]{1,0:T(8,128)(2,1)} %bitcast.9, bf16[512,4096]{1,0:T(8,128)(2,1)} %bitcast.10), custom_call_target="tpu_custom_call" | custom-call | tf_op jit(solution)/shard_map/products/pallas_call | solution.py:533

commit v4 on v3

--- a/solution.py
+++ b/solution.py
@@ -13,7 +13,7 @@
 REPLICA = ("ry", "rx")
 FSDP = ("z", "x", "c")
 BF = jnp.bfloat16
-NS, NR, EARLY, LEAD, LATE, PARTS = 24, 232, 7, 21, 4, 2
+NS, NR, EARLY, LEAD, LATE, PARTS = 24, 232, 7, 19, 4, 2
 F32 = jnp.float32
 
 

time: 123 us -> 124 us (level)
  no operation moved by 1% of the time
where the time goes in v4:
time: 124 us
  Pallas kernels  123 us (99%)
    pallas_call x1, Pallas kernels, fused(): pl.pallas_call(functools.partial(kernel, sizes, scale), out_shape=[jax.Sh...  117 us
    pallas_call x1, Pallas kernels, products(): pl.pallas_call(products_kernel, grid=(PARTS,), out_shape=[jax.ShapeDtypeS...  6.59 us

profile of v4, /device:TPU:1, one launch (start us, length us, event | category | flops | bytes accessed | tf_op | source)
XLA Modules:
  0.0 123.9 jit_solution(9624387356660206693)
XLA Ops:
  0.6 116.7 %step.1 = (bf16[32,16,4096]{2,1,0:T(8,128)(2,1)}, bf16[32,16,4096]{2,1,0:T(8,128)(2,1)}, bf16[224,512]{1,0:T(8,128)(2,1)}, bf16[448,512]{1,0:T(8,128)(2,1)}) custom-call(s32[8]{0:T(128)} %refs_0_.1, bf16[16,4096]{1,0:T(8,128)(2,1)} %bitcast.14, bf16[224,4096]{1,0:T(8,128)(2,1)} %bitcast.11, bf16[224,4096]{1,0:T(8,128)(2,1)} %bitcast.12, ...), custom_call_target="tpu_custom_call" | custom-call | tf_op jit(solution)/shard_map/step/pallas_call | solution.py:471
  117.3 6.6 %products.1 = (bf16[224,4096]{1,0:T(8,128)(2,1)}, bf16[224,4096]{1,0:T(8,128)(2,1)}, bf16[224,4096]{1,0:T(8,128)(2,1)}) custom-call(bf16[224,512]{1,0:T(8,128)(2,1)} %get-tuple-element.10.hidden_t, bf16[448,512]{1,0:T(8,128)(2,1)} %get-tuple-element.11.d_both_t, bf16[512,4096]{1,0:T(8,128)(2,1)} %bitcast.9, bf16[512,4096]{1,0:T(8,128)(2,1)} %bitcast.10), custom_call_target="tpu_custom_call" | custom-call | tf_op jit(solution)/shard_map/products/pallas_call | solution.py:533
